TPU v7x, 256 devices: a whole 4x4x8 slice. The times are simulated.
256 devices in a mesh: tok: 16 (over z, core), voc: 16 (over x, y).
Axes of the slice: x: 4, y: 4, z: 8, core: 2. Of those that a mesh axis runs over, the one named last changes fastest.
Arguments:
- hidden: bfloat16 [8192, 1024], P('tok'), may hold values from -64 to 64
- head_weight: bfloat16 [1024, 65536], P('tok', 'voc'), may hold values from -1 to 1
- target_logits: bfloat16 [8192, 65536], P('tok', 'voc'), may hold values from -320 to 320
- token_ids: int32 [8192], P('tok'), may hold values from 0 to 65535
Outputs:
- loss: float32 [], replicated
- grad_hidden: float32 [8192, 1024], P('tok', 'voc')
- grad_head: float32 [1024, 65536], P('tok', 'voc')
All inputs are finite; a program needn't handle non-finite values.
Results may differ from a plain program's by a relative error of at most 0.015.
Values may be sent and summed in bfloat16 or wider, within the bound.
A program may use at most 128 MiB of HBM per device.

v0:
```python
import functools

import jax
import jax.numpy as jnp
from jax import lax
from jax.sharding import Mesh
from jax.sharding import PartitionSpec as P

VOC = ("voc_0", "voc_1")
TOK = ("tok_0", "tok_1")
TOK_VOC = ("tok_0", "tok_1", "voc_0", "voc_1")


ce_weight = 0.5


def from_everyone(x, axis):
    devices = lax.axis_size(axis)
    return lax.all_to_all(jnp.broadcast_to(x[None], (devices, *x.shape)), axis, 0, 0, tiled=True)


def gathered_once(x, axis):
    leaves = jax.tree.leaves(x)
    sequence = sorted(range(len(leaves)), key=lambda k: -leaves[k].size)
    width = (1, *leaves[sequence[0]].shape)[-1]
    lines = [
        jnp.pad(leaves[k].reshape(-1), (0, -leaves[k].size % width)).reshape(-1, width)
        for k in sequence
    ]
    both, at, found = (from_everyone(jnp.concatenate(lines), axis), 0, {})
    for k, line in zip(sequence, lines):
        share = both[:, at : at + len(line)].reshape(len(both), -1)
        found[k] = share[:, : leaves[k].size].reshape(-1, *leaves[k].shape)
        at += len(line)
    numbers = iter(range(len(leaves)))
    return jax.tree.map(lambda _: found[next(numbers)], x)


def combined_pairwise(pieces, combine):
    while len(jax.tree.leaves(pieces)[0]) > 1:
        pieces = jax.vmap(combine)(
            *(jax.tree.map(lambda part: part[side::2], pieces) for side in (0, 1))
        )
    return jax.tree.map(lambda part: part[0], pieces)


def joined_all(x, axis, combine):
    pieces = gathered_once(x, axis)
    return combined_pairwise(pieces, combine)


def over_axes(x, axes):
    return functools.reduce(lax.psum, axes, x)


def split_up(x, dim, devices):
    lengths = x.shape
    pieces = x.reshape(*lengths[:dim], devices, lengths[dim] // devices, *lengths[dim + 1 :])
    return jnp.moveaxis(pieces, dim, 0)


def sum_at_owner(x, axis, dim):
    pieces = split_up(x, dim, lax.axis_size(axis))
    arrived = lax.all_to_all(pieces, axis, split_axis=0, concat_axis=0, tiled=True)
    return arrived.astype(jnp.float32).sum(axis=0)


def pair_stats(left, right):
    t_max = jnp.maximum(left[0], right[0])
    t_sum = left[1] * jnp.exp(left[0] - t_max) + right[1] * jnp.exp(right[0] - t_max)
    z_max = jnp.maximum(left[2], right[2])
    z_sum = left[3] * jnp.exp(left[2] - z_max) + right[3] * jnp.exp(right[2] - z_max)
    return (t_max, t_sum, z_max, z_sum)


def body(hidden, head_weight, target_logits, token_ids):
    rows = hidden.shape[0]
    share = head_weight.shape[1]
    vocab_start = lax.axis_index(VOC) * share
    whole = lax.all_gather(head_weight, TOK, axis=0, tiled=True)
    draft = jnp.dot(hidden, whole, preferred_element_type=jnp.float32)
    target = target_logits.astype(jnp.float32)
    local_t = jnp.max(target, axis=1)
    local_z = jnp.max(draft, axis=1)
    target_exp = jnp.exp(target - local_t[:, None])
    draft_exp = jnp.exp(draft - local_z[:, None])
    merged = joined_all(
        (local_t, jnp.sum(target_exp, axis=1), local_z, jnp.sum(draft_exp, axis=1)), VOC, pair_stats
    )
    target_max, target_sum, draft_max, draft_sum = merged
    target_exp = target_exp * jnp.exp(local_t - target_max)[:, None]
    draft_exp = draft_exp * jnp.exp(local_z - draft_max)[:, None]
    probs_p = target_exp / target_sum[:, None]
    probs_q = draft_exp / draft_sum[:, None]
    lse_t = target_max + jnp.log(target_sum)
    lse_z = draft_max + jnp.log(draft_sum)
    column = lax.broadcasted_iota(jnp.int32, (rows, share), 1) + vocab_start
    own = (column == token_ids[:, None]).astype(jnp.float32)
    voc_count = lax.axis_size(VOC)
    per_token = jnp.sum(probs_p * (target - draft) - ce_weight * own * draft, axis=1)
    per_token = per_token + ((1.0 + ce_weight) * lse_z - lse_t) / voc_count
    total = over_axes(jnp.sum(per_token), TOK_VOC)
    loss = total / (rows * lax.axis_size(TOK))
    slope = ((1.0 + ce_weight) * probs_q - probs_p - ce_weight * own).astype(jnp.bfloat16)
    partial_grad = lax.dot_general(
        slope, whole, (((1,), (1,)), ((), ())), preferred_element_type=jnp.float32
    )
    grad_hidden = sum_at_owner(partial_grad.astype(jnp.bfloat16), VOC, 1)
    grad_head = lax.psum_scatter(
        lax.dot_general(
            hidden, slope, (((0,), (0,)), ((), ())), preferred_element_type=jnp.float32
        ).astype(jnp.bfloat16),
        TOK,
        scatter_dimension=0,
        tiled=True,
    ).astype(jnp.float32)
    return (loss, grad_hidden, grad_head)


def solution(mesh):
    torus = Mesh(mesh.devices.reshape(8, 2, 4, 4), ("tok_0", "tok_1", "voc_0", "voc_1"))
    return jax.shard_map(
        body,
        mesh=torus,
        in_specs=(P(TOK, None), P(TOK, VOC), P(TOK, VOC), P(TOK)),
        out_specs=(P(), P(TOK, VOC), P(TOK, VOC)),
        check_vma=False,
    )
```

profile of v0, /device:TPU:1, one launch (start us, length us, event | category | flops | bytes accessed | tf_op | source)
XLA Modules:
  0.0 202.9 jit_solution(14382294832241544402)
XLA Ops:
  7.2 0.7 all-gather.2.cloned.1.call-update
  7.9 2.8 %reduce_max.27 = bf16[512]{0:T(512)(128)(2,1)S(1)} reduce(bf16[512,4096]{1,0:T(8,128)(2,1)} %param.6, bf16[]{:T(256)} %constant.11.clone.1), dimensions={1}, to_apply=%region_0.0 | reduce | flops 2096640 | bytes 4195330 | tf_op jit(solution)/shard_map/reduce_max | solution.py:83
  10.7 3.7 %fusion.2 = f32[512]{0:T(512)S(1)} fusion(bf16[512,4096]{1,0:T(8,128)(2,1)} %param.6, f32[512]{0:T(512)S(1)} %reduce_max.28), kind=kLoop, calls=%fused_computation.6 | loop fusion | flops 6290944 | bytes 4198400 | tf_op jit(solution)/shard_map/reduce_sum | solution.py:88
  14.4 55.5 %all-gather.2.cloned.1.call-done = bf16[1024,4096]{1,0:T(8,128)(2,1)} async-done(((bf16[64,4096]{1,0:T(8,128)(2,1)}), bf16[1024,4096]{1,0:T(8,128)(2,1)}) %all-gather.2.cloned.1.call-update) | async-done | bytes 8388624 | tf_op jit(solution)/shard_map/all_gather | solution.py:80
  69.9 7.0 %fusion.12 = (f32[512]{0:T(512)S(1)}, f32[512,4096]{1,0:T(8,128)S(1)}) fusion(bf16[512,1024]{1,0:T(8,128)(2,1)S(1)} %copy-done, bf16[1024,4096]{1,0:T(8,128)(2,1)} %all-gather.2.cloned.1.call-done), kind=kOutput, calls=%fused_computation.41 | convolution fusion | flops 4297063936 | bytes 17827840 | tf_op jit(solution)/shard_map/dot_general | solution.py:81
  77.0 3.2 %copy-done.1 = f32[512,4096]{1,0:T(8,128)} copy-done((f32[512,4096]{1,0:T(8,128)}, f32[512,4096]{1,0:T(8,128)S(1)}, u32[]{:S(2)}) %copy-start.1) | copy-done | bytes 8388632
  80.2 1.3 fusion.8
  82.1 6.5 %all-to-all-start = ((f32[16,4,512]{2,1,0:T(4,128)}), f32[16,4,512]{2,1,0:T(4,128)S(1)}, u32[]{:S(2)}, u32[]{:S(2)}) async-start(f32[16,4,512]{2,1,0:T(4,128)} %broadcast_in_dim.2), calls=%async_computation | async-start | bytes 262144 | tf_op jit(solution)/shard_map/all_to_all | solution.py:19
  88.9 6.5 %all-to-all-done = f32[16,4,512]{2,1,0:T(4,128)S(1)} async-done(((f32[16,4,512]{2,1,0:T(4,128)}), f32[16,4,512]{2,1,0:T(4,128)S(1)}, u32[]{:S(2)}, u32[]{:S(2)}) %all-to-all-start) | async-done | bytes 131104 | tf_op jit(solution)/shard_map/all_to_all | solution.py:19
  96.2 10.7 %fusion.7 = (bf16[512,4096]{1,0:T(8,128)(2,1)S(1)}, f32[512]{0:T(512)S(1)}) fusion(f32[512,4096]{1,0:T(8,128)} %copy-done.1, f32[512]{0:T(512)S(1)} %bitcast.30, f32[512]{0:T(512)S(1)} %subtract_exponential_fusion.1, s32[4096]{0:T(1024)S(1)} %iota_add_fusion, f32[512]{0:T(512)S(1)} %get-tuple-element.34, s32[512]{0:T(512)S(1)} %copy-done.3, ...), kind=kLoop, calls=%fused_computation.11 | loop fusion | flops 37748224 | bytes 16809984 | tf_op jit(solution)/shard_map/convert_element_type | solution.py:104
  107.0 2.0 copy-done.2
  109.0 6.8 %convert_bitcast_fusion = bf16[1024,4096]{0,1:T(8,128)(2,1)} fusion(bf16[512,4096]{1,0:T(8,128)(2,1)S(1)} %get-tuple-element.28, bf16[512,1024]{1,0:T(8,128)(2,1)S(1)} %copy-done), kind=kOutput, calls=%fused_computation.12 | convolution fusion | flops 4299161600 | bytes 13631488 | tf_op jit(solution)/shard_map/dot_general | solution.py:110
  115.7 11.5 %copy.18 = bf16[1024,4096]{1,0:T(8,128)(2,1)} copy(bf16[1024,4096]{0,1:T(8,128)(2,1)} %convert_bitcast_fusion) | data formatting | bytes 16777216
  127.2 9.2 %convolution_convert_fusion = bf16[512,1024]{1,0:T(8,128)(2,1)S(1)} fusion(bf16[512,4096]{1,0:T(8,128)(2,1)} %copy-done.2, bf16[1024,4096]{1,0:T(8,128)(2,1)} %all-gather.2.cloned.1.call-done), kind=kOutput, calls=%fused_computation.16 | convolution fusion | flops 4295491584 | bytes 13631488 | tf_op jit(solution)/shard_map/dot_general | solution.py:105
  136.4 1.3 copy.16
  137.7 3.7 %all-to-all-start.1 = ((bf16[16,512,64]{1,2,0:T(8,128)(2,1)}), bf16[16,512,64]{1,2,0:T(8,128)(2,1)S(1)}, u32[]{:S(2)}, u32[]{:S(2)}) async-start(bf16[16,512,64]{1,2,0:T(8,128)(2,1)} %bitcast.11), calls=%async_computation.1 | async-start | bytes 2097152 | tf_op jit(solution)/shard_map/all_to_all | solution.py:64
  142.0 13.7 %psum.28 = f32[]{:T(128)} all-reduce(f32[]{:T(128)} %add_reduce_fusion), channel_id=1, replica_groups=mesh['tok_0'=8,'tok_1'=2,'voc_0'=4,'voc_1'=4] {'tok_0'}, use_global_device_ids=true, to_apply=%region_6.7 | all-reduce | flops 1 | bytes 8 | tf_op jit(solution)/shard_map/psum | solution.py:53
  155.7 7.0 %psum.29 = f32[]{:T(128)} all-reduce(f32[]{:T(128)} %psum.28), channel_id=1, replica_groups=mesh['tok_0'=8,'tok_1'=2,'voc_0'=4,'voc_1'=4] {'tok_1'}, use_global_device_ids=true, to_apply=%region_7.8 | all-reduce | flops 1 | bytes 8 | tf_op jit(solution)/shard_map/psum | solution.py:53
  162.7 9.7 %psum.30 = f32[]{:T(128)} all-reduce(f32[]{:T(128)} %psum.29), channel_id=1, replica_groups=mesh['tok_0'=8,'tok_1'=2,'voc_0'=4,'voc_1'=4] {'voc_0'}, use_global_device_ids=true, to_apply=%region_8.9 | all-reduce | flops 1 | bytes 8 | tf_op jit(solution)/shard_map/psum | solution.py:53
  172.4 9.9 %psum.31 = f32[]{:T(128)} all-reduce(f32[]{:T(128)} %psum.30), channel_id=1, replica_groups=mesh['tok_0'=8,'tok_1'=2,'voc_0'=4,'voc_1'=4] {'voc_1'}, use_global_device_ids=true, to_apply=%region_9.10 | all-reduce | flops 1 | bytes 8 | tf_op jit(solution)/shard_map/psum | solution.py:53
  183.0 0.8 convert_reduce_fusion
  183.8 8.3 %reduce-scatter.4.cloned.1.call-done = bf16[64,4096]{1,0:T(8,128)(2,1)} async-done(((bf16[1024,4096]{1,0:T(8,128)(2,1)}), bf16[64,4096]{1,0:T(8,128)(2,1)}) %reduce-scatter.4.cloned.1.call-update) | async-done | bytes 524304
  192.1 1.5 copy.19
  193.6 1.3 copy.17
  (52 shorter events, 2.4 us)
Async XLA Ops:
  7.2 62.7 %copy-start = (bf16[512,1024]{1,0:T(8,128)(2,1)S(1)}, bf16[512,1024]{1,0:T(8,128)(2,1)}, u32[]{:S(2)}) copy-start(bf16[512,1024]{1,0:T(8,128)(2,1)} %param.4) | copy-start | bytes 3145732
  7.2 62.7 %all-gather.2.cloned.1.call-start = ((), (), s32[]{:S(2)}) async-start(), calls=%async_computation.3 | async-start | bytes 8912896 | tf_op jit(solution)/shard_map/all_gather | solution.py:80
  76.9 3.2 %copy-start.1 = (f32[512,4096]{1,0:T(8,128)}, f32[512,4096]{1,0:T(8,128)S(1)}, u32[]{:S(2)}) copy-start(f32[512,4096]{1,0:T(8,128)S(1)} %get-tuple-element.35) | copy-start | bytes 25165828
  77.0 19.3 %copy-start.3 = (s32[512]{0:T(512)S(1)}, s32[512]{0:T(512)}, u32[]{:S(2)}) copy-start(s32[512]{0:T(512)} %param.7) | copy-start | bytes 6148
  82.1 13.2 %all-to-all-start = ((f32[16,4,512]{2,1,0:T(4,128)}), f32[16,4,512]{2,1,0:T(4,128)S(1)}, u32[]{:S(2)}, u32[]{:S(2)}) async-start(f32[16,4,512]{2,1,0:T(4,128)} %broadcast_in_dim.2), calls=%async_computation | async-start | bytes 262144 | tf_op jit(solution)/shard_map/all_to_all | solution.py:19
  88.7 103.5 %reduce-scatter.4.cloned.1.call-start = ((), (), s32[]{:S(2)}) async-start(), calls=%async_computation.4 | async-start | bytes 8912896
  107.0 2.0 copy-start.2
  137.7 45.2 %all-to-all-start.1 = ((bf16[16,512,64]{1,2,0:T(8,128)(2,1)}), bf16[16,512,64]{1,2,0:T(8,128)(2,1)S(1)}, u32[]{:S(2)}, u32[]{:S(2)}) async-start(bf16[16,512,64]{1,2,0:T(8,128)(2,1)} %bitcast.11), calls=%async_computation.1 | async-start | bytes 2097152 | tf_op jit(solution)/shard_map/all_to_all | solution.py:64
Sparse Core Ops, SparseCore 0:
  9.8 60.0 all-gather.1
  127.3 64.7 reduce-scatter.3
where the time goes:
time: 206 us; the launch traced here: 203 us
  waiting for transfers between devices  71 us (34%)
  blocking collectives  40.3 us (20%)
  matrix products  23 us (11%)
  local copies, waits for them, and re-layouts  22.1 us (11%)
  other arithmetic  20.1 us (10%)
  between operations  16 us (8%)
  starting transfers between devices  10.4 us (5%)
    all_gather x1, waiting for transfers between devices, body(): whole = lax.all_gather(head_weight, TOK, axis=0, tiled=True)  55.5 us
    psum x4, blocking collectives, over_axes(): return functools.reduce(lax.psum, axes, x)  40.3 us
    unnamed x12, local copies, waits for them, and re-layouts  19.5 us
    convert_element_type x1, other arithmetic, body(): ((1.0 + ce_weight) * probs_q - probs_p - ce_weight * own).astype(jnp.bflo...  10.7 us
    dot_general x1, matrix products, body(): lax.dot_general(slope, whole, (((1,), (1,)), ((), ())), preferred_element...  9.18 us
    unnamed x3, waiting for transfers between devices  9.04 us
    dot_general x1, matrix products, body(): draft = jnp.dot(hidden, whole, preferred_element_type=jnp.float32)  7.05 us
    dot_general x1, matrix products, body(): lax.dot_general(hidden, slope, (((0,), (0,)), ((), ())), preferred_elemen...  6.75 us
  transfers between devices with their start and end apart: 4, of which 3 were waited for; matrix products, arithmetic and copies ran while one was open for 9% of the time, Pallas kernels for 0%

commit v1 on v0

v1 whole, which is shorter than its diff:
```python
import functools

import jax
import jax.numpy as jnp
from jax import lax
from jax.experimental import pallas as pl
from jax.experimental.pallas import tpu as pltpu
from jax.sharding import Mesh
from jax.sharding import PartitionSpec as P

VOC = ("voc_0", "voc_1")
TOK = ("tok_0", "tok_1")
CE = 0.5
F32 = jnp.float32
BF16 = jnp.bfloat16
MESH = pl.DeviceIdType.MESH
ROWS = 32
LOW = -1e30


def kernel(dims, *refs):
    Z, X, Y, T, D, V, NS = dims
    NV = X * Y
    NB = 2 * NS
    W = V // NB
    RB = D // (2 * Z)
    G = W // 128
    NE = (Z - 1) * NS
    NC = Z * NS
    (
        hid_hbm, head_hbm, tgt_hbm, ids_ref,
        loss_out, gh_out, gw_out,
        hg, hid, hid_t, tgt, zed, base, slope,
        part, sib_out, sib_in, ring_out, ring_in, gh_send, gh_recv,
        st_t, st_z, run_m, run_s, ids_c, m_c, s_c, own_t, lsum, row_t,
        l_xy, l_sib, l_z,
        in_sem, ag_s, ag_r, sb_s, sb_r, so_sem,
        rs_s, rs_r, rb_s, rb_r, gh_s, gh_r, tt_s, tt_r, zz_s, zz_r,
        lx_s, lx_r, lz_s, lz_r, lb_sem,
    ) = refs
    z = lax.axis_index("tok_0")
    c = lax.axis_index("tok_1")
    x = lax.axis_index("voc_0")
    y = lax.axis_index("voc_1")
    me = x * Y + y
    sib = 1 - c
    right = lax.rem(z + 1, Z)
    left = lax.rem(z + Z - 1, Z)
    toward = ({"tok_0": right}, {"tok_0": left})
    other = {"tok_1": sib}

    def plane(k):
        j = lax.rem(me + k, NV)
        return j, {"voc_0": j // Y, "voc_1": lax.rem(j, Y)}

    def remote(src, dst, s, r, device):
        return pltpu.make_async_remote_copy(
            src_ref=src, dst_ref=dst, send_sem=s, recv_sem=r, device_id=device, device_id_type=MESH
        )

    mine = 2 * z + c

    def in_head(b):
        return pltpu.make_async_copy(head_hbm.at[:, pl.ds(b * W, W)], hg.at[mine, b], in_sem.at[b])

    def in_hid(k):
        return pltpu.make_async_copy(
            hid_hbm.at[:, pl.ds(k * 2 * RB, 2 * RB)], hid.at[k], in_sem.at[NB + k]
        )

    def in_tgt(b):
        return pltpu.make_async_copy(
            tgt_hbm.at[:, pl.ds(b * W, W)], tgt.at[b], in_sem.at[NB + Z + b]
        )

    for b in range(NB):
        in_head(b).start()
    for k in range(Z):
        in_hid(k).start()
    for b in range(NB):
        in_tgt(b).start()

    barrier = pltpu.get_barrier_semaphore()
    for device in (*toward, other):
        pl.semaphore_signal(barrier, inc=1, device_id=device, device_id_type=MESH)
    for k in range(1, NV):
        pl.semaphore_signal(barrier, inc=1, device_id=plane(k)[1], device_id_type=MESH)
    pl.semaphore_wait(barrier, 3 + NV - 1)

    def chip_at(way, s):
        return lax.rem(z + Z - s, Z) if way == 0 else lax.rem(z + s, Z)

    def ag(way, n):
        slot = hg.at[2 * chip_at(way, n // NS) + c, way * NS + lax.rem(n, NS)]
        return remote(slot, slot, ag_s.at[way, n], ag_r.at[way, n], toward[way])

    def ag_in(way, n):
        slot = hg.at[2 * chip_at(way, n // NS + 1) + c, way * NS + lax.rem(n, NS)]
        return remote(slot, slot, ag_s.at[way, n], ag_r.at[way, n], toward[way])

    def sb(way, n, core):
        slot = hg.at[2 * chip_at(way, n // NS + 1) + core, way * NS + lax.rem(n, NS)]
        return remote(slot, slot, sb_s.at[way, n], sb_r.at[way, n], other)

    def shard(core):
        slot = hg.at[2 * z + core]
        return remote(slot, slot, so_sem.at[0], so_sem.at[1], other)

    for i in range(NS):
        for way in range(2):
            in_head(way * NS + i).wait()
            ag(way, i).start()
    shard(c).start()

    @pl.loop(0, NB)
    def _(b):
        zed[b] = jnp.zeros((T, W), F32)

    @pl.loop(0, Z)
    def _(k):
        in_hid(k).wait()
        hid_t[k] = hid[k].T

    def column(row):
        return jnp.broadcast_to(row, (128, T)).T

    ids_c[...] = column(ids_ref[...].astype(F32))

    def reset():
        run_m[...] = jnp.full((T, 128), LOW, F32)
        run_s[...] = jnp.zeros((T, 128), F32)

    reset()
    own_t[...] = jnp.zeros((ROWS, W), F32)
    lsum[...] = jnp.zeros((ROWS, W), F32)

    def groups(v):
        return [v[:, g * 128 : (g + 1) * 128] for g in range(G)]

    def stats(load):
        @pl.loop(0, T // ROWS)
        def _(k):
            at = pl.ds(pl.multiple_of(k * ROWS, ROWS), ROWS)
            cols = groups(load(at))
            old = run_m[at]
            new = functools.reduce(jnp.maximum, cols, old)
            total = run_s[at] * jnp.exp(old - new)
            run_s[at] = total + functools.reduce(jnp.add, [jnp.exp(v - new) for v in cols])
            run_m[at] = new

    def local_stats():
        m = run_m[...].T
        top = jnp.max(m, axis=0, keepdims=True)
        return top, jnp.sum(run_s[...].T * jnp.exp(m - top), axis=0, keepdims=True)

    def st(ref, s, r, k):
        return remote(ref.at[me], ref.at[me], s.at[k], r.at[me], plane(k)[1])

    def st_in(ref, s, r, k):
        j, device = plane(k)
        return remote(ref.at[j], ref.at[j], s.at[k], r.at[j], device)

    def send_stats(ref, s, r):
        top, total = local_stats()
        ref[me] = jnp.concatenate([top, total], axis=0)
        for k in range(1, NV):
            st(ref, s, r, k).start()

    def joined_stats(ref, s, r):
        for k in range(1, NV):
            st_in(ref, s, r, k).wait_recv()
        all_m = jnp.concatenate([ref[j][0:1] for j in range(NV)], axis=0)
        all_s = jnp.concatenate([ref[j][1:2] for j in range(NV)], axis=0)
        top = jnp.max(all_m, axis=0, keepdims=True)
        return top, jnp.sum(all_s * jnp.exp(all_m - top), axis=0, keepdims=True)

    lane = lax.broadcasted_iota(jnp.int32, (ROWS, W), 1)

    def wide(v):
        return jnp.concatenate([v] * G, axis=1)

    def fill_base(b):
        col = (lane + (me * V + b * W)).astype(F32)

        @pl.loop(0, T // ROWS)
        def _(k):
            at = pl.ds(pl.multiple_of(k * ROWS, ROWS), ROWS)
            t = tgt[b, at].astype(F32)
            p = jnp.exp(t - wide(m_c[at])) * wide(s_c[at])
            own = col == wide(ids_c[at])
            base[b, at] = jnp.where(own, p + CE, p)
            own_t[...] += jnp.where(own, t, 0.0)

    def draft(m):
        s = m // NS + 1
        for way in range(2):
            b = way * NS + lax.rem(m, NS)
            chips = (chip_at(way, s - 1), chip_at(way, s))
            lhs = jnp.concatenate([hid[k] for k in chips], axis=1)
            rhs = jnp.concatenate([hg[2 * k + e, b] for k in chips for e in range(2)], axis=0)
            zed[b] += jnp.dot(lhs, rhs, preferred_element_type=F32)

    def arrive(n):
        for way in range(2):
            ag_in(way, n).wait_recv()

            @pl.when(n + NS < NE)
            def _():
                ag(way, n + NS).start()

            sb(way, n, c).start()

    def arrived(m):
        for way in range(2):
            sb(way, m, sib).wait_recv()

    for b in range(NB):
        in_tgt(b).wait()
    shard(sib).wait_recv()

    LAST = NE - NS

    @pl.loop(0, LAST + 1)
    def _(n):
        arrive(n)
        s = n // NS + 1
        i = lax.rem(n, NS)

        @pl.when(n > 0)
        def _():
            arrived(n - 1)

        @pl.when((n > 0) & (lax.rem((n - 1) // NS, 2) == 0) & (n < LAST + 1))
        def _():
            draft(n - 1)

        @pl.when(s == 2)
        def _():
            for way in range(2):
                stats(lambda at: tgt[way * NS + i, at].astype(F32))

        @pl.when((s == 3) & (i == 0))
        def _():
            send_stats(st_t, tt_s, tt_r)
            reset()

        @pl.when((s == 4) & (i == NS - 1))
        def _():
            top, total = joined_stats(st_t, tt_s, tt_r)
            m_c[...] = column(top)
            s_c[...] = column(1.0 / total)
            row_t[...] = top + jnp.log(total)

        @pl.when(s == Z - 2)
        def _():
            for way in range(2):
                fill_base(way * NS + i)

    @pl.loop(LAST + 1, NE + 1)
    def _(n):
        @pl.when(n < NE)
        def _():
            arrive(n)

        arrived(n - 1)
        draft(n - 1)
        for way in range(2):
            b = way * NS + lax.rem(n - 1, NS)
            stats(lambda at: zed[b, at])

    send_stats(st_z, zz_s, zz_r)
    top_z, total_z = joined_stats(st_z, zz_s, zz_r)
    m_c[...] = column(top_z)
    s_c[...] = column((1.0 + CE) / total_z)
    row_t[...] = ((1.0 + CE) * (top_z + jnp.log(total_z)) - row_t[...]) * (1.0 / NV)

    def fill_slope(b):
        @pl.loop(0, T // ROWS)
        def _(k):
            at = pl.ds(pl.multiple_of(k * ROWS, ROWS), ROWS)
            q = jnp.exp(zed[b, at] - wide(m_c[at])) * wide(s_c[at])
            slope[b, at] = (q - base[b, at]).astype(BF16)

    def rb(way, n):
        return remote(
            sib_out.at[way, n], sib_in.at[way, n], rb_s.at[way, n], rb_r.at[way, n], other
        )

    def rs(way, n):
        return remote(
            ring_out.at[way, n], ring_in.at[way, n], rs_s.at[way, n], rs_r.at[way, n], toward[way]
        )

    def compute(n):
        s = n // NS
        slot = lax.rem(n, 2)
        for way in range(2):
            b = way * NS + lax.rem(n, NS)
            got = jnp.dot(hid_t[chip_at(way, s + 1)], slope[b], preferred_element_type=F32)
            part[slot, way, 0] = got[:RB]
            part[slot, way, 1] = got[RB:]
            sib_out[way, n] = part[slot, way, sib].astype(BF16)
            rb(way, n).start()

    def finish(n):
        s = n // NS
        slot = lax.rem(n, 2)
        for way in range(2):
            rb(way, n).wait_recv()

            @pl.when(s == 0)
            def _():
                val = part[slot, way, c] + sib_in[way, n].astype(F32)
                ring_out[way, n] = val.astype(BF16)
                rs(way, n).start()

            @pl.when(s > 0)
            def _():
                rs(way, n - NS).wait_recv()
                val = (part[slot, way, c] + sib_in[way, n].astype(F32)) + ring_in[
                    way, n - NS
                ].astype(F32)

                @pl.when(s < Z - 1)
                def _():
                    ring_out[way, n] = val.astype(BF16)
                    rs(way, n).start()

                @pl.when(s == Z - 1)
                def _():
                    b = way * NS + lax.rem(n, NS)
                    gw_out[:, pl.ds(pl.multiple_of(b * W, W), W)] = val

    def gh(j):
        device = {"voc_0": j // Y, "voc_1": lax.rem(j, Y)}
        return remote(gh_send.at[j], gh_recv.at[me], gh_s.at[j], gh_r.at[me], device)

    def gh_in(k):
        j, device = plane(k)
        return remote(gh_send.at[j], gh_recv.at[j], gh_s.at[j], gh_r.at[j], device)

    def hidden_part(e):
        r = lax.rem(e + me // 2, Z)
        acc = jnp.zeros((2 * RB, T), F32)
        for b in range(NB):
            lhs = jnp.concatenate([hg[2 * r, b], hg[2 * r + 1, b]], axis=0)
            acc = acc + lax.dot_general(
                lhs, slope[b], (((1,), (1,)), ((), ())), preferred_element_type=F32
            )
        for e2 in range(2):
            gh_send[2 * r + e2] = acc[e2 * RB : (e2 + 1) * RB].astype(BF16)

            @pl.when(2 * r + e2 != me)
            def _():
                gh(2 * r + e2).start()

    def loss_part(b):
        @pl.loop(0, T // ROWS)
        def _(k):
            at = pl.ds(pl.multiple_of(k * ROWS, ROWS), ROWS)
            lsum[...] += base[b, at] * (tgt[b, at].astype(F32) - zed[b, at])

    def total_of(v):
        return jnp.sum(jnp.sum(v, axis=0, keepdims=True), axis=1, keepdims=True)

    def sib_loss():
        return remote(l_sib.at[0], l_sib.at[1], lb_sem.at[0], lb_sem.at[1], other)

    def ring_loss(k):
        slot = l_z.at[chip_at(0, k)]
        return remote(slot, slot, lz_s.at[k], lz_r.at[k], toward[0])

    def ring_loss_in(k):
        slot = l_z.at[chip_at(0, k + 1)]
        return remote(slot, slot, lz_s.at[k], lz_r.at[k], toward[0])

    @pl.loop(0, NC + 1)
    def _(n):
        @pl.when(n < NS)
        def _():
            for way in range(2):
                fill_slope(way * NS + n)

        @pl.when(n < NC)
        def _():
            compute(n)

        @pl.when(n > 0)
        def _():
            finish(n - 1)

        @pl.when((n >= NS + 1) & (n < NS + 1 + 2 * Z) & (lax.rem(n - NS - 1, 2) == 0))
        def _():
            hidden_part((n - NS - 1) // 2)

        @pl.when((n >= NS) & (n < 2 * NS))
        def _():
            for way in range(2):
                loss_part(way * NS + lax.rem(n, NS))

        @pl.when(n == 2 * NS)
        def _():
            local = total_of(lsum[...] - CE * own_t[...]) + total_of(row_t[...])
            l_xy[me] = jnp.broadcast_to(local, (8, 128))
            for k in range(1, NV):
                st(l_xy, lx_s, lx_r, k).start()

        @pl.when(n == 3 * NS - 1)
        def _():
            for k in range(1, NV):
                st_in(l_xy, lx_s, lx_r, k).wait_recv()
            l_sib[0] = functools.reduce(jnp.add, [l_xy[j] for j in range(NV)])
            sib_loss().start()

        @pl.when(n == 3 * NS)
        def _():
            sib_loss().wait_recv()
            l_z[z] = l_sib[0] + l_sib[1]
            ring_loss(0).start()

        @pl.when((n > 3 * NS) & (n <= 3 * NS + 2 * (Z - 1)) & (lax.rem(n - 3 * NS, 2) == 0))
        def _():
            k = (n - 3 * NS) // 2
            ring_loss_in(k - 1).wait_recv()

            @pl.when(k < Z - 1)
            def _():
                ring_loss(k).start()

    loss_out[...] = functools.reduce(jnp.add, [l_z[k] for k in range(Z)]) * (1.0 / (2 * Z * T))
    for k in range(1, NV):
        gh_in(k).wait_recv()
    gh_recv[me] = gh_send[me]
    gh_out[...] = functools.reduce(jnp.add, [gh_recv[j].astype(F32) for j in range(NV)])

    shard(c).wait_send()
    sib_loss().wait_send()

    @pl.loop(0, NE)
    def _(n):
        for way in range(2):
            ag(way, n).wait_send()
            sb(way, n, c).wait_send()
            rs(way, n).wait_send()

    @pl.loop(0, NC)
    def _(n):
        for way in range(2):
            rb(way, n).wait_send()

    @pl.loop(0, Z - 1)
    def _(k):
        ring_loss(k).wait_send()

    for k in range(1, NV):
        st(st_t, tt_s, tt_r, k).wait_send()
        st(st_z, zz_s, zz_r, k).wait_send()
        st(l_xy, lx_s, lx_r, k).wait_send()
        gh_in(k).wait_send()


def body(dims, hidden, head, target, ids):
    Z, X, Y, T, D, V, NS = dims
    NV = X * Y
    NB = 2 * NS
    W = V // NB
    RB = D // (2 * Z)
    NE, NC = (Z - 1) * NS, Z * NS
    vmem, dma = pltpu.VMEM, pltpu.SemaphoreType.DMA
    hbm = pl.BlockSpec(memory_space=pltpu.HBM)
    local = pl.BlockSpec(memory_space=pltpu.VMEM)
    loss, gh, gw = pl.pallas_call(
        functools.partial(kernel, dims),
        out_shape=(
            jax.ShapeDtypeStruct((8, 128), F32),
            jax.ShapeDtypeStruct((RB, T), F32),
            jax.ShapeDtypeStruct((RB, V), F32),
        ),
        in_specs=[hbm, hbm, hbm, local],
        out_specs=(local, local, local),
        scratch_shapes=[
            vmem((2 * Z, NB, RB, W), BF16),
            vmem((Z, T, 2 * RB), BF16),
            vmem((Z, 2 * RB, T), BF16),
            vmem((NB, T, W), BF16),
            vmem((NB, T, W), F32),
            vmem((NB, T, W), F32),
            vmem((NB, T, W), BF16),
            vmem((2, 2, 2, RB, W), F32),
            vmem((2, NC, RB, W), BF16),
            vmem((2, NC, RB, W), BF16),
            vmem((2, NE, RB, W), BF16),
            vmem((2, NE, RB, W), BF16),
            vmem((NV, RB, T), BF16),
            vmem((NV, RB, T), BF16),
            vmem((NV, 2, T), F32),
            vmem((NV, 2, T), F32),
            vmem((T, 128), F32),
            vmem((T, 128), F32),
            vmem((T, 128), F32),
            vmem((T, 128), F32),
            vmem((T, 128), F32),
            vmem((ROWS, W), F32),
            vmem((ROWS, W), F32),
            vmem((1, T), F32),
            vmem((NV, 8, 128), F32),
            vmem((2, 8, 128), F32),
            vmem((Z, 8, 128), F32),
            dma((2 * NB + Z,)),
            dma((2, NE)), dma((2, NE)),
            dma((2, NE)), dma((2, NE)),
            dma((2,)),
            dma((2, NE)), dma((2, NE)),
            dma((2, NC)), dma((2, NC)),
            dma((NV,)), dma((NV,)),
            dma((NV,)), dma((NV,)),
            dma((NV,)), dma((NV,)),
            dma((NV,)), dma((NV,)),
            dma((Z,)), dma((Z,)),
            dma((2,)),
        ],
        compiler_params=pltpu.CompilerParams(
            collective_id=0, has_side_effects=True, vmem_limit_bytes=63 * 1024 * 1024
        ),
        name="step",
    )(hidden, head, target, ids.reshape(1, T))
    return loss[0, 0], gh.T, gw


def solution(mesh):
    sizes = mesh.shape
    tok, voc = sizes["tok"], sizes["voc"]
    side = {16: 4, 8: 4, 4: 2}[voc]
    Z, X, Y = tok // 2, side, voc // side
    torus = Mesh(mesh.devices.reshape(Z, 2, X, Y), TOK + VOC)

    def whole(hidden, head, target, ids):
        dims = (Z, X, Y, hidden.shape[0] // tok, hidden.shape[1], head.shape[1] // voc, 4)
        return jax.shard_map(
            functools.partial(body, dims),
            mesh=torus,
            in_specs=(P(TOK, None), P(TOK, VOC), P(TOK, VOC), P(TOK)),
            out_specs=(P(), P(TOK, VOC), P(TOK, VOC)),
            check_vma=False,
        )(hidden, head, target, ids)

    return whole
```

time: 206 us -> 125 us (0.61); the launches traced: 203 us -> 125 us
  Pallas kernels: 0 us -> 119 us
  waiting for transfers between devices: 71 us -> 0 us
  blocking collectives: 40.3 us -> 0 us
  matrix products: 23 us -> 0 us
  other arithmetic: 20.1 us -> 0 us
  local copies, waits for them, and re-layouts: 22.1 us -> 5.02 us
  between operations: 16 us -> 0.64 us
  starting transfers between devices: 10.4 us -> 0 us
    pallas_call x0 -> x1, Pallas kernels: none -> 119 us  [body(): pl.pallas_call(functools.partial(kernel, dims), out_shape=(jax.ShapeDtype...]
    all_gather x1 -> x0, waiting for transfers between devices: 55.5 us -> none  [body(): whole = lax.all_gather(head_weight, TOK, axis=0, tiled=True)]
    psum x4 -> x0, blocking collectives: 40.3 us -> none  [over_axes(): return functools.reduce(lax.psum, axes, x)]
    dot_general x3 -> x0, matrix products: 23 us -> none  [the longest x1 9.18 us: body(): lax.dot_general(slope, whole, (((1,), (1,)), ((), ())), preferred_element...]
    unnamed x12 -> x2, local copies, waits for them, and re-layouts: 19.5 us -> 3.84 us
    convert_element_type x1 -> x0, other arithmetic: 10.7 us -> none  [body(): ((1.0 + ce_weight) * probs_q - probs_p - ce_weight * own).astype(jnp.bflo...]
    all_to_all x2 -> x0, starting transfers between devices: 10.2 us -> none  [the longest x1 6.53 us: from_everyone(): lax.all_to_all(jnp.broadcast_to(x[None], (devices, *x.shape)), axis, 0, 0...]
    unnamed x3 -> x0, waiting for transfers between devices: 9.04 us -> none
  transfers between devices with their start and end apart: 4 -> 0, of which waited for: 3 -> 0; matrix products, arithmetic and copies ran while one was open for 9% -> 0% of each run, Pallas kernels for 0% -> 0%
where the time goes in v1:
time: 125 us
  Pallas kernels  119 us (95%)
  local copies, waits for them, and re-layouts  5.02 us (4%)
    pallas_call x1, Pallas kernels, body(): pl.pallas_call(functools.partial(kernel, dims), out_shape=(jax.ShapeDtype...  119 us
    unnamed x2, local copies, waits for them, and re-layouts  3.84 us

profile of v1, /device:TPU:1, one launch (start us, length us, event | category | flops | bytes accessed | tf_op | source)
XLA Modules:
  0.0 124.8 jit_solution(6070426467046340973)
XLA Ops:
  0.6 119.1 %step.1 = (f32[8,128]{1,0:T(8,128)}, f32[64,512]{1,0:T(8,128)}, f32[64,4096]{1,0:T(8,128)}) custom-call(bf16[512,1024]{1,0:T(8,128)(2,1)} %refs_0_.1, bf16[64,4096]{1,0:T(8,128)(2,1)} %refs_1_.1, bf16[512,4096]{1,0:T(8,128)(2,1)} %refs_2_.1, s32[1,512]{1,0:T(1,128)} %bitcast.4), custom_call_target="tpu_custom_call" | custom-call | tf_op jit(solution)/shard_map/step/pallas_call | solution.py:472
  119.8 1.2 slice.3
  121.0 1.6 %copy.9 = f32[512,64]{0,1:T(8,128)} copy(f32[512,64]{0,1:T(8,128)} %bitcast.3) | data formatting | bytes 262144
  122.5 2.3 %copy.10 = f32[64,4096]{1,0:T(8,128)} copy(f32[64,4096]{1,0:T(8,128)} %get-tuple-element.14) | data formatting | bytes 2097152

commit v2 on v1

--- a/solution.py
+++ b/solution.py
@@ -27,14 +27,16 @@
     G = W // 128
     NE = (Z - 1) * NS
     NC = Z * NS
+    NA = NS // 2
+    NG = (Z - 2) * NA
     (
-        hid_hbm, head_hbm, tgt_hbm, ids_ref,
+        hid_hbm, head_hbm, tgt_hbm, ids_hbm,
         loss_out, gh_out, gw_out,
-        hg, hid, hid_t, tgt, zed, base, slope,
+        ids_ref, hg, hid, hid_t, tgt, zed, base, slope,
         part, sib_out, sib_in, ring_out, ring_in, gh_send, gh_recv,
-        st_t, st_z, run_m, run_s, ids_c, m_c, s_c, own_t, lsum, row_t,
+        gh_acc, st_t, st_z, run_m, run_s, ids_c, m_c, s_c, own_t, lsum, row_t,
         l_xy, l_sib, l_z,
-        in_sem, ag_s, ag_r, sb_s, sb_r, so_sem,
+        in_sem, ready, ag_s, ag_r, al_s, al_r, sb_s, sb_r, sl_s, sl_r, so_sem,
         rs_s, rs_r, rb_s, rb_r, gh_s, gh_r, tt_s, tt_r, zz_s, zz_r,
         lx_s, lx_r, lz_s, lz_r, lb_sem,
     ) = refs
@@ -73,44 +75,58 @@
             tgt_hbm.at[:, pl.ds(b * W, W)], tgt.at[b], in_sem.at[NB + Z + b]
         )
 
-    for b in range(NB):
-        in_head(b).start()
+    in_ids = pltpu.make_async_copy(ids_hbm, ids_ref, in_sem.at[2 * NB + Z])
+    for i in range(NS):
+        for way in range(2):
+            in_head(way * NS + i).start()
+    in_ids.start()
     for k in range(Z):
         in_hid(k).start()
     for b in range(NB):
         in_tgt(b).start()
 
     barrier = pltpu.get_barrier_semaphore()
-    for device in (*toward, other):
+    row = [{"voc_0": lax.rem(x + k, X)} for k in range(1, X)]
+    line = [{"voc_1": lax.rem(y + k, Y)} for k in range(1, Y)]
+    near = (*toward, other, *row, *line)
+    for device in near:
         pl.semaphore_signal(barrier, inc=1, device_id=device, device_id_type=MESH)
-    for k in range(1, NV):
-        pl.semaphore_signal(barrier, inc=1, device_id=plane(k)[1], device_id_type=MESH)
-    pl.semaphore_wait(barrier, 3 + NV - 1)
+    pl.semaphore_wait(barrier, len(near))
 
     def chip_at(way, s):
         return lax.rem(z + Z - s, Z) if way == 0 else lax.rem(z + s, Z)
 
-    def ag(way, n):
-        slot = hg.at[2 * chip_at(way, n // NS) + c, way * NS + lax.rem(n, NS)]
+    def pair(way, n, s, core):
+        return hg.at[2 * chip_at(way, s) + core, pl.ds(way * NS + 2 * lax.rem(n, NA), 2)]
+
+    def ag(way, n, s):
+        slot = pair(way, n, s, c)
         return remote(slot, slot, ag_s.at[way, n], ag_r.at[way, n], toward[way])
 
-    def ag_in(way, n):
-        slot = hg.at[2 * chip_at(way, n // NS + 1) + c, way * NS + lax.rem(n, NS)]
-        return remote(slot, slot, ag_s.at[way, n], ag_r.at[way, n], toward[way])
-
     def sb(way, n, core):
-        slot = hg.at[2 * chip_at(way, n // NS + 1) + core, way * NS + lax.rem(n, NS)]
+        slot = pair(way, n, n // NA + 1, core)
         return remote(slot, slot, sb_s.at[way, n], sb_r.at[way, n], other)
+
+    def al(way, i, s):
+        slot = hg.at[2 * chip_at(way, s) + c, way * NS + i]
+        return remote(slot, slot, al_s.at[way, i], al_r.at[way, i], toward[way])
+
+    def sl(way, i, core):
+        slot = hg.at[2 * chip_at(way, Z - 1) + core, way * NS + i]
+        return remote(slot, slot, sl_s.at[way, i], sl_r.at[way, i], other)
 
     def shard(core):
         slot = hg.at[2 * z + core]
         return remote(slot, slot, so_sem.at[0], so_sem.at[1], other)
 
-    for i in range(NS):
-        for way in range(2):
-            in_head(way * NS + i).wait()
-            ag(way, i).start()
+    for i in range(NA):
+        for way in range(2):
+            for e in range(2):
+                in_head(way * NS + 2 * i + e).wait()
+            ag(way, i, 0).start()
     shard(c).start()
+    for device in row:
+        pl.semaphore_signal(ready, inc=1, device_id=device, device_id_type=MESH)
 
     @pl.loop(0, NB)
     def _(b):
@@ -124,6 +140,7 @@
     def column(row):
         return jnp.broadcast_to(row, (128, T)).T
 
+    in_ids.wait()
     ids_c[...] = column(ids_ref[...].astype(F32))
 
     def reset():
@@ -191,60 +208,64 @@
             base[b, at] = jnp.where(own, p + CE, p)
             own_t[...] += jnp.where(own, t, 0.0)
 
-    def draft(m):
-        s = m // NS + 1
-        for way in range(2):
-            b = way * NS + lax.rem(m, NS)
-            chips = (chip_at(way, s - 1), chip_at(way, s))
-            lhs = jnp.concatenate([hid[k] for k in chips], axis=1)
-            rhs = jnp.concatenate([hg[2 * k + e, b] for k in chips for e in range(2)], axis=0)
-            zed[b] += jnp.dot(lhs, rhs, preferred_element_type=F32)
-
-    def arrive(n):
-        for way in range(2):
-            ag_in(way, n).wait_recv()
-
-            @pl.when(n + NS < NE)
-            def _():
-                ag(way, n + NS).start()
-
-            sb(way, n, c).start()
-
-    def arrived(m):
-        for way in range(2):
-            sb(way, m, sib).wait_recv()
+    def draft(s, b, way):
+        chips = (chip_at(way, s - 1), chip_at(way, s))
+        lhs = jnp.concatenate([hid[k] for k in chips], axis=1)
+        rhs = jnp.concatenate([hg[2 * k + e, b] for k in chips for e in range(2)], axis=0)
+        zed[b] += jnp.dot(lhs, rhs, preferred_element_type=F32)
 
     for b in range(NB):
         in_tgt(b).wait()
     shard(sib).wait_recv()
 
-    LAST = NE - NS
-
-    @pl.loop(0, LAST + 1)
+    @pl.loop(0, NG + 1)
     def _(n):
-        arrive(n)
-        s = n // NS + 1
-        i = lax.rem(n, NS)
+        s = n // NA + 1
+        i = lax.rem(n, NA)
+
+        @pl.when(n < NG)
+        def _():
+            for way in range(2):
+                ag(way, n, s).wait_recv()
+
+                @pl.when(n + NA < NG)
+                def _():
+                    ag(way, n + NA, s).start()
+
+                @pl.when(n + NA >= NG)
+                def _():
+                    for e in range(2):
+                        al(way, 2 * i + e, s).start()
+
+                sb(way, n, c).start()
 
         @pl.when(n > 0)
         def _():
-            arrived(n - 1)
-
-        @pl.when((n > 0) & (lax.rem((n - 1) // NS, 2) == 0) & (n < LAST + 1))
-        def _():
-            draft(n - 1)
+            m = n - 1
+            for way in range(2):
+                sb(way, m, sib).wait_recv()
+
+            @pl.when(lax.rem(m // NA, 2) == 0)
+            def _():
+                @pl.loop(0, 2)
+                def _(e):
+                    for way in range(2):
+                        draft(m // NA + 1, way * NS + 2 * lax.rem(m, NA) + e, way)
 
         @pl.when(s == 2)
         def _():
-            for way in range(2):
-                stats(lambda at: tgt[way * NS + i, at].astype(F32))
+            @pl.loop(0, 2)
+            def _(e):
+                for way in range(2):
+                    stats(lambda at: tgt[way * NS + 2 * i + e, at].astype(F32))
 
         @pl.when((s == 3) & (i == 0))
         def _():
+            pl.semaphore_wait(ready, X - 1)
             send_stats(st_t, tt_s, tt_r)
             reset()
 
-        @pl.when((s == 4) & (i == NS - 1))
+        @pl.when((s == 4) & (i == NA - 1))
         def _():
             top, total = joined_stats(st_t, tt_s, tt_r)
             m_c[...] = column(top)
@@ -253,20 +274,27 @@
 
         @pl.when(s == Z - 2)
         def _():
+            @pl.loop(0, 2)
+            def _(e):
+                for way in range(2):
+                    fill_base(way * NS + 2 * i + e)
+
+    @pl.loop(0, NS + 1)
+    def _(i):
+        @pl.when(i < NS)
+        def _():
             for way in range(2):
-                fill_base(way * NS + i)
-
-    @pl.loop(LAST + 1, NE + 1)
-    def _(n):
-        @pl.when(n < NE)
-        def _():
-            arrive(n)
-
-        arrived(n - 1)
-        draft(n - 1)
-        for way in range(2):
-            b = way * NS + lax.rem(n - 1, NS)
-            stats(lambda at: zed[b, at])
+                al(way, i, Z - 1).wait_recv()
+                sl(way, i, c).start()
+
+        @pl.when(i > 0)
+        def _():
+            for way in range(2):
+                sl(way, i - 1, sib).wait_recv()
+            for way in range(2):
+                b = way * NS + i - 1
+                draft(Z - 1, b, way)
+                stats(lambda at: zed[b, at])
 
     send_stats(st_z, zz_s, zz_r)
     top_z, total_z = joined_stats(st_z, zz_s, zz_r)
@@ -340,19 +368,35 @@
         return remote(gh_send.at[j], gh_recv.at[j], gh_s.at[j], gh_r.at[j], device)
 
     def hidden_part(e):
-        r = lax.rem(e + me // 2, Z)
-        acc = jnp.zeros((2 * RB, T), F32)
-        for b in range(NB):
-            lhs = jnp.concatenate([hg[2 * r, b], hg[2 * r + 1, b]], axis=0)
-            acc = acc + lax.dot_general(
-                lhs, slope[b], (((1,), (1,)), ((), ())), preferred_element_type=F32
+        r = lax.rem(e // 4 + me // 4, NV // 4)
+        q = lax.rem(e, 4)
+        got = []
+        for k in range(NB // 4):
+            b = q * (NB // 4) + k
+            lhs = jnp.concatenate([hg[4 * r + i, b] for i in range(4)], axis=0)
+            got.append(
+                lax.dot_general(
+                    lhs, slope[b], (((1,), (1,)), ((), ())), preferred_element_type=F32
+                )
             )
-        for e2 in range(2):
-            gh_send[2 * r + e2] = acc[e2 * RB : (e2 + 1) * RB].astype(BF16)
-
-            @pl.when(2 * r + e2 != me)
-            def _():
-                gh(2 * r + e2).start()
+        got = functools.reduce(jnp.add, got)
+
+        @pl.when(q == 0)
+        def _():
+            gh_acc[...] = got
+
+        @pl.when(q > 0)
+        def _():
+            gh_acc[...] += got
+
+        @pl.when(q == 3)
+        def _():
+            for i in range(4):
+                gh_send[4 * r + i] = gh_acc[i * RB : (i + 1) * RB].astype(BF16)
+
+                @pl.when(4 * r + i != me)
+                def _():
+                    gh(4 * r + i).start()
 
     def loss_part(b):
         @pl.loop(0, T // ROWS)
@@ -389,9 +433,9 @@
         def _():
             finish(n - 1)
 
-        @pl.when((n >= NS + 1) & (n < NS + 1 + 2 * Z) & (lax.rem(n - NS - 1, 2) == 0))
-        def _():
-            hidden_part((n - NS - 1) // 2)
+        @pl.when((n >= 2 * NS) & (n < 2 * NS + NV))
+        def _():
+            hidden_part(n - 2 * NS)
 
         @pl.when((n >= NS) & (n < 2 * NS))
         def _():
@@ -436,11 +480,21 @@
     shard(c).wait_send()
     sib_loss().wait_send()
 
+    @pl.loop(0, NG)
+    def _(n):
+        for way in range(2):
+            ag(way, n, 0).wait_send()
+            sb(way, n, c).wait_send()
+
+    @pl.loop(0, NS)
+    def _(i):
+        for way in range(2):
+            al(way, i, 0).wait_send()
+            sl(way, i, c).wait_send()
+
     @pl.loop(0, NE)
     def _(n):
         for way in range(2):
-            ag(way, n).wait_send()
-            sb(way, n, c).wait_send()
             rs(way, n).wait_send()
 
     @pl.loop(0, NC)
@@ -457,6 +511,18 @@
         st(st_z, zz_s, zz_r, k).wait_send()
         st(l_xy, lx_s, lx_r, k).wait_send()
         gh_in(k).wait_send()
+
+
+def hand_over(loss, gh, gw, loss_out, gh_out, gw_out, sems):
+    copies = [
+        pltpu.make_async_copy(src, dst, sems.at[k])
+        for k, (src, dst) in enumerate(((gw, gw_out), (gh, gh_out)))
+    ]
+    for copy in copies:
+        copy.start()
+    loss_out[...] = loss[0:1, 0:1]
+    for copy in copies:
+        copy.wait()
 
 
 def body(dims, hidden, head, target, ids):
@@ -465,20 +531,21 @@
     NB = 2 * NS
     W = V // NB
     RB = D // (2 * Z)
-    NE, NC = (Z - 1) * NS, Z * NS
+    NE, NC, NG = (Z - 1) * NS, Z * NS, (Z - 2) * NS // 2
     vmem, dma = pltpu.VMEM, pltpu.SemaphoreType.DMA
     hbm = pl.BlockSpec(memory_space=pltpu.HBM)
     local = pl.BlockSpec(memory_space=pltpu.VMEM)
     loss, gh, gw = pl.pallas_call(
         functools.partial(kernel, dims),
         out_shape=(
-            jax.ShapeDtypeStruct((8, 128), F32),
-            jax.ShapeDtypeStruct((RB, T), F32),
-            jax.ShapeDtypeStruct((RB, V), F32),
+            vmem((8, 128), F32),
+            vmem((RB, T), F32),
+            vmem((RB, V), F32),
         ),
-        in_specs=[hbm, hbm, hbm, local],
+        in_specs=[hbm, hbm, hbm, hbm],
         out_specs=(local, local, local),
         scratch_shapes=[
+            vmem((1, T), jnp.int32),
             vmem((2 * Z, NB, RB, W), BF16),
             vmem((Z, T, 2 * RB), BF16),
             vmem((Z, 2 * RB, T), BF16),
@@ -493,6 +560,7 @@
             vmem((2, NE, RB, W), BF16),
             vmem((NV, RB, T), BF16),
             vmem((NV, RB, T), BF16),
+            vmem((4 * RB, T), F32),
             vmem((NV, 2, T), F32),
             vmem((NV, 2, T), F32),
             vmem((T, 128), F32),
@@ -506,9 +574,12 @@
             vmem((NV, 8, 128), F32),
             vmem((2, 8, 128), F32),
             vmem((Z, 8, 128), F32),
-            dma((2 * NB + Z,)),
-            dma((2, NE)), dma((2, NE)),
-            dma((2, NE)), dma((2, NE)),
+            dma((2 * NB + Z + 1,)),
+            pltpu.SemaphoreType.REGULAR,
+            dma((2, NG)), dma((2, NG)),
+            dma((2, NS)), dma((2, NS)),
+            dma((2, NG)), dma((2, NG)),
+            dma((2, NS)), dma((2, NS)),
             dma((2,)),
             dma((2, NE)), dma((2, NE)),
             dma((2, NC)), dma((2, NC)),
@@ -520,11 +591,24 @@
             dma((2,)),
         ],
         compiler_params=pltpu.CompilerParams(
-            collective_id=0, has_side_effects=True, vmem_limit_bytes=63 * 1024 * 1024
+            collective_id=0, has_side_effects=True, vmem_limit_bytes=58 * 1024 * 1024
         ),
         name="step",
     )(hidden, head, target, ids.reshape(1, T))
-    return loss[0, 0], gh.T, gw
+    loss, gh, gw = pl.pallas_call(
+        hand_over,
+        out_shape=(
+            jax.ShapeDtypeStruct((1, 1), F32),
+            jax.ShapeDtypeStruct((RB, T), F32),
+            jax.ShapeDtypeStruct((RB, V), F32),
+        ),
+        in_specs=[local] * 3,
+        out_specs=(local, hbm, hbm),
+        scratch_shapes=[dma((3,))],
+        compiler_params=pltpu.CompilerParams(vmem_limit_bytes=4 * 1024 * 1024),
+        name="hand_over",
+    )(loss, gh, gw)
+    return loss.reshape(()), gh.T, gw
 
 
 def solution(mesh):

time: 125 us -> 115 us (0.920)
  local copies, waits for them, and re-layouts: 5.02 us -> 0 us
  Pallas kernels: 119 us -> 114 us
    pallas_call x1 -> x2, Pallas kernels: 119 us -> 114 us  [the longest x1 113 us: body(): pl.pallas_call(functools.partial(kernel, dims), out_shape=(vmem((8, 128),...]
    unnamed x2 -> x0, local copies, waits for them, and re-layouts: 3.84 us -> none
where the time goes in v2:
time: 115 us
  Pallas kernels  114 us (99%)
    pallas_call x1, Pallas kernels, body(): pl.pallas_call(functools.partial(kernel, dims), out_shape=(vmem((8, 128),...  113 us

profile of v2, /device:TPU:1, one launch (start us, length us, event | category | flops | bytes accessed | tf_op | source)
XLA Modules:
  0.0 114.9 jit_solution(8373151010079251629)
XLA Ops:
  0.6 112.7 %step.1 = (f32[8,128]{1,0:T(8,128)S(1)}, f32[64,512]{1,0:T(8,128)S(1)}, f32[64,4096]{1,0:T(8,128)S(1)}) custom-call(bf16[512,1024]{1,0:T(8,128)(2,1)} %refs_0_.1, bf16[64,4096]{1,0:T(8,128)(2,1)} %refs_1_.1, bf16[512,4096]{1,0:T(8,128)(2,1)} %refs_2_.1, s32[1,512]{1,0:T(1,128)} %bitcast.3), custom_call_target="tpu_custom_call" | custom-call | tf_op jit(solution)/shard_map/step/pallas_call | solution.py:538
  113.4 1.5 %hand_over.1 = (f32[1,1]{1,0:T(1,128)}, f32[64,512]{1,0:T(8,128)}, f32[64,4096]{1,0:T(8,128)}) custom-call(f32[8,128]{1,0:T(8,128)S(1)} %get-tuple-element.9.loss, f32[64,512]{1,0:T(8,128)S(1)} %get-tuple-element.10.gh, f32[64,4096]{1,0:T(8,128)S(1)} %get-tuple-element.11.gw), custom_call_target="tpu_custom_call" | custom-call | tf_op jit(solution)/shard_map/hand_over/pallas_call | solution.py:598

commit v3 on v2

--- a/solution.py
+++ b/solution.py
@@ -15,6 +15,7 @@
 BF16 = jnp.bfloat16
 MESH = pl.DeviceIdType.MESH
 ROWS = 32
+UNROLL = 4
 LOW = -1e30
 
 
@@ -25,10 +26,9 @@
     W = V // NB
     RB = D // (2 * Z)
     G = W // 128
-    NE = (Z - 1) * NS
-    NC = Z * NS
     NA = NS // 2
     NG = (Z - 2) * NA
+    NC = Z * NA
     (
         hid_hbm, head_hbm, tgt_hbm, ids_hbm,
         loss_out, gh_out, gw_out,
@@ -37,7 +37,7 @@
         gh_acc, st_t, st_z, run_m, run_s, ids_c, m_c, s_c, own_t, lsum, row_t,
         l_xy, l_sib, l_z,
         in_sem, ready, ag_s, ag_r, al_s, al_r, sb_s, sb_r, sl_s, sl_r, so_sem,
-        rs_s, rs_r, rb_s, rb_r, gh_s, gh_r, tt_s, tt_r, zz_s, zz_r,
+        rl_s, rl_r, rs_s, rs_r, bl_s, bl_r, rb_s, rb_r, gh_s, gh_r, tt_s, tt_r, zz_s, zz_r,
         lx_s, lx_r, lz_s, lz_r, lb_sem,
     ) = refs
     z = lax.axis_index("tok_0")
@@ -154,10 +154,15 @@
     def groups(v):
         return [v[:, g * 128 : (g + 1) * 128] for g in range(G)]
 
+    def rowwise(step):
+        @pl.loop(0, T // (ROWS * UNROLL))
+        def _(k):
+            for u in range(UNROLL):
+                step(pl.ds(pl.multiple_of((k * UNROLL + u) * ROWS, ROWS), ROWS))
+
     def stats(load):
-        @pl.loop(0, T // ROWS)
-        def _(k):
-            at = pl.ds(pl.multiple_of(k * ROWS, ROWS), ROWS)
+        @rowwise
+        def _(at):
             cols = groups(load(at))
             old = run_m[at]
             new = functools.reduce(jnp.maximum, cols, old)
@@ -186,10 +191,9 @@
     def joined_stats(ref, s, r):
         for k in range(1, NV):
             st_in(ref, s, r, k).wait_recv()
-        all_m = jnp.concatenate([ref[j][0:1] for j in range(NV)], axis=0)
-        all_s = jnp.concatenate([ref[j][1:2] for j in range(NV)], axis=0)
-        top = jnp.max(all_m, axis=0, keepdims=True)
-        return top, jnp.sum(all_s * jnp.exp(all_m - top), axis=0, keepdims=True)
+        rows = [ref[j] for j in range(NV)]
+        top = functools.reduce(jnp.maximum, [v[0:1] for v in rows])
+        return top, functools.reduce(jnp.add, [v[1:2] * jnp.exp(v[0:1] - top) for v in rows])
 
     lane = lax.broadcasted_iota(jnp.int32, (ROWS, W), 1)
 
@@ -199,9 +203,8 @@
     def fill_base(b):
         col = (lane + (me * V + b * W)).astype(F32)
 
-        @pl.loop(0, T // ROWS)
-        def _(k):
-            at = pl.ds(pl.multiple_of(k * ROWS, ROWS), ROWS)
+        @rowwise
+        def _(at):
             t = tgt[b, at].astype(F32)
             p = jnp.exp(t - wide(m_c[at])) * wide(s_c[at])
             own = col == wide(ids_c[at])
@@ -303,61 +306,88 @@
     row_t[...] = ((1.0 + CE) * (top_z + jnp.log(total_z)) - row_t[...]) * (1.0 / NV)
 
     def fill_slope(b):
-        @pl.loop(0, T // ROWS)
-        def _(k):
-            at = pl.ds(pl.multiple_of(k * ROWS, ROWS), ROWS)
+        @rowwise
+        def _(at):
             q = jnp.exp(zed[b, at] - wide(m_c[at])) * wide(s_c[at])
             slope[b, at] = (q - base[b, at]).astype(BF16)
 
+    def rl(way, i):
+        return remote(
+            ring_out.at[way, 0, i], ring_in.at[way, 0, i], rl_s.at[way, i], rl_r.at[way, i], toward[way]
+        )
+
+    def bl(way, i):
+        return remote(
+            sib_out.at[way, 0, i], sib_in.at[way, 0, i], bl_s.at[way, i], bl_r.at[way, i], other
+        )
+
+    def both(n):
+        return n // NA, pl.ds(2 * lax.rem(n, NA), 2)
+
+    def rs(way, n):
+        at = both(n)
+        return remote(
+            ring_out.at[way, *at], ring_in.at[way, *at], rs_s.at[way, n], rs_r.at[way, n], toward[way]
+        )
+
     def rb(way, n):
+        at = both(n)
         return remote(
-            sib_out.at[way, n], sib_in.at[way, n], rb_s.at[way, n], rb_r.at[way, n], other
-        )
-
-    def rs(way, n):
-        return remote(
-            ring_out.at[way, n], ring_in.at[way, n], rs_s.at[way, n], rs_r.at[way, n], toward[way]
-        )
+            sib_out.at[way, *at], sib_in.at[way, *at], rb_s.at[way, n], rb_r.at[way, n], other
+        )
+
+    def product(way, s, i, own):
+        got = jnp.dot(
+            hid_t[chip_at(way, s + 1)], slope[way * NS + i], preferred_element_type=F32
+        )
+        own[0] = got[:RB]
+        own[1] = got[RB:]
+        sib_out[way, s, i] = own[sib].astype(BF16)
 
     def compute(n):
-        s = n // NS
-        slot = lax.rem(n, 2)
-        for way in range(2):
-            b = way * NS + lax.rem(n, NS)
-            got = jnp.dot(hid_t[chip_at(way, s + 1)], slope[b], preferred_element_type=F32)
-            part[slot, way, 0] = got[:RB]
-            part[slot, way, 1] = got[RB:]
-            sib_out[way, n] = part[slot, way, sib].astype(BF16)
+        for way in range(2):
+            for e in range(2):
+                product(way, n // NA, 2 * lax.rem(n, NA) + e, part.at[lax.rem(n, 2), way, e])
             rb(way, n).start()
 
+    def finish_first(i):
+        for way in range(2):
+            bl(way, i).wait_recv()
+            val = part[lax.rem(i, 2), way, 0, c] + sib_in[way, 0, i].astype(F32)
+            ring_out[way, 0, i] = val.astype(BF16)
+            rl(way, i).start()
+
     def finish(n):
-        s = n // NS
-        slot = lax.rem(n, 2)
+        s = n // NA
         for way in range(2):
             rb(way, n).wait_recv()
 
-            @pl.when(s == 0)
+            @pl.when(s == 1)
             def _():
-                val = part[slot, way, c] + sib_in[way, n].astype(F32)
-                ring_out[way, n] = val.astype(BF16)
-                rs(way, n).start()
-
-            @pl.when(s > 0)
+                for e in range(2):
+                    rl(way, 2 * lax.rem(n, NA) + e).wait_recv()
+
+            @pl.when(s > 1)
             def _():
-                rs(way, n - NS).wait_recv()
-                val = (part[slot, way, c] + sib_in[way, n].astype(F32)) + ring_in[
-                    way, n - NS
-                ].astype(F32)
+                rs(way, n - NA).wait_recv()
+
+            for e in range(2):
+                i = 2 * lax.rem(n, NA) + e
+                own = part[lax.rem(n, 2), way, e, c] + sib_in[way, s, i].astype(F32)
+                val = own + ring_in[way, s - 1, i].astype(F32)
 
                 @pl.when(s < Z - 1)
                 def _():
-                    ring_out[way, n] = val.astype(BF16)
-                    rs(way, n).start()
+                    ring_out[way, s, i] = val.astype(BF16)
 
                 @pl.when(s == Z - 1)
                 def _():
-                    b = way * NS + lax.rem(n, NS)
-                    gw_out[:, pl.ds(pl.multiple_of(b * W, W), W)] = val
+                    at = pl.ds(pl.multiple_of((way * NS + i) * W, W), W)
+                    gw_out[:, at] = val
+
+            @pl.when(s < Z - 1)
+            def _():
+                rs(way, n).start()
 
     def gh(j):
         device = {"voc_0": j // Y, "voc_1": lax.rem(j, Y)}
@@ -399,9 +429,8 @@
                     gh(4 * r + i).start()
 
     def loss_part(b):
-        @pl.loop(0, T // ROWS)
-        def _(k):
-            at = pl.ds(pl.multiple_of(k * ROWS, ROWS), ROWS)
+        @rowwise
+        def _(at):
             lsum[...] += base[b, at] * (tgt[b, at].astype(F32) - zed[b, at])
 
     def total_of(v):
@@ -418,99 +447,137 @@
         slot = l_z.at[chip_at(0, k + 1)]
         return remote(slot, slot, lz_s.at[k], lz_r.at[k], toward[0])
 
-    @pl.loop(0, NC + 1)
+    def sent():
+        shard(c).wait_send()
+
+        @pl.loop(0, NG)
+        def _(n):
+            for way in range(2):
+                ag(way, n, 0).wait_send()
+                sb(way, n, c).wait_send()
+
+        @pl.loop(0, NS)
+        def _(i):
+            for way in range(2):
+                al(way, i, 0).wait_send()
+                sl(way, i, c).wait_send()
+
+        for k in range(1, NV):
+            st(st_t, tt_s, tt_r, k).wait_send()
+            st(st_z, zz_s, zz_r, k).wait_send()
+
+    def gathered():
+        loss_out[...] = functools.reduce(jnp.add, [l_z[k] for k in range(Z)]) * (
+            1.0 / (2 * Z * T)
+        )
+        for k in range(1, NV):
+            gh_in(k).wait_recv()
+        gh_recv[me] = gh_send[me]
+
+        @pl.loop(0, RB // 16)
+        def _(k):
+            at = pl.ds(pl.multiple_of(k * 16, 16), 16)
+            gh_out[at] = functools.reduce(jnp.add, [gh_recv[j, at].astype(F32) for j in range(NV)])
+
+        sib_loss().wait_send()
+
+        @pl.loop(0, Z - 1)
+        def _(k):
+            ring_loss(k).wait_send()
+
+        for k in range(1, NV):
+            st(l_xy, lx_s, lx_r, k).wait_send()
+            gh_in(k).wait_send()
+
+    @pl.loop(0, NS)
+    def _(i):
+        for way in range(2):
+            fill_slope(way * NS + i)
+            product(way, 0, i, part.at[lax.rem(i, 2), way, 0])
+            bl(way, i).start()
+
+        @pl.when(i > 0)
+        def _():
+            finish_first(i - 1)
+
+    @pl.loop(NA, NC + 1)
     def _(n):
-        @pl.when(n < NS)
-        def _():
-            for way in range(2):
-                fill_slope(way * NS + n)
-
         @pl.when(n < NC)
         def _():
             compute(n)
 
-        @pl.when(n > 0)
+        @pl.when(n == NA)
+        def _():
+            finish_first(NS - 1)
+
+        @pl.when(n > NA)
         def _():
             finish(n - 1)
 
-        @pl.when((n >= 2 * NS) & (n < 2 * NS + NV))
-        def _():
-            hidden_part(n - 2 * NS)
-
-        @pl.when((n >= NS) & (n < 2 * NS))
-        def _():
-            for way in range(2):
-                loss_part(way * NS + lax.rem(n, NS))
-
-        @pl.when(n == 2 * NS)
+        @pl.when(n == NA + 1)
+        def _():
+            sent()
+
+        @pl.when((n > NA) & (n <= NA + 2))
+        def _():
+            @pl.loop(0, NB // 2)
+            def _(k):
+                loss_part((n - NA - 1) * (NB // 2) + k)
+
+        @pl.when(n == NA + 3)
         def _():
             local = total_of(lsum[...] - CE * own_t[...]) + total_of(row_t[...])
             l_xy[me] = jnp.broadcast_to(local, (8, 128))
             for k in range(1, NV):
                 st(l_xy, lx_s, lx_r, k).start()
 
-        @pl.when(n == 3 * NS - 1)
+        @pl.when((n >= NA + 3) & (n < NA + 3 + NV // 2))
+        def _():
+            @pl.loop(0, 2)
+            def _(e):
+                hidden_part(2 * (n - NA - 3) + e)
+
+        @pl.when(n == NA + 4)
         def _():
             for k in range(1, NV):
                 st_in(l_xy, lx_s, lx_r, k).wait_recv()
             l_sib[0] = functools.reduce(jnp.add, [l_xy[j] for j in range(NV)])
             sib_loss().start()
 
-        @pl.when(n == 3 * NS)
+        @pl.when(n == NA + 5)
         def _():
             sib_loss().wait_recv()
             l_z[z] = l_sib[0] + l_sib[1]
             ring_loss(0).start()
 
-        @pl.when((n > 3 * NS) & (n <= 3 * NS + 2 * (Z - 1)) & (lax.rem(n - 3 * NS, 2) == 0))
-        def _():
-            k = (n - 3 * NS) // 2
+        @pl.when((n > NA + 5) & (n <= NA + 5 + Z - 1))
+        def _():
+            k = n - NA - 5
             ring_loss_in(k - 1).wait_recv()
 
             @pl.when(k < Z - 1)
             def _():
                 ring_loss(k).start()
 
-    loss_out[...] = functools.reduce(jnp.add, [l_z[k] for k in range(Z)]) * (1.0 / (2 * Z * T))
-    for k in range(1, NV):
-        gh_in(k).wait_recv()
-    gh_recv[me] = gh_send[me]
-    gh_out[...] = functools.reduce(jnp.add, [gh_recv[j].astype(F32) for j in range(NV)])
-
-    shard(c).wait_send()
-    sib_loss().wait_send()
-
-    @pl.loop(0, NG)
-    def _(n):
-        for way in range(2):
-            ag(way, n, 0).wait_send()
-            sb(way, n, c).wait_send()
+        @pl.when(n == NC - 1)
+        def _():
+            gathered()
 
     @pl.loop(0, NS)
     def _(i):
         for way in range(2):
-            al(way, i, 0).wait_send()
-            sl(way, i, c).wait_send()
-
-    @pl.loop(0, NE)
+            rl(way, i).wait_send()
+            bl(way, i).wait_send()
+
+    @pl.loop(NA, NC - NA)
     def _(n):
         for way in range(2):
             rs(way, n).wait_send()
 
-    @pl.loop(0, NC)
+    @pl.loop(NA, NC)
     def _(n):
         for way in range(2):
             rb(way, n).wait_send()
-
-    @pl.loop(0, Z - 1)
-    def _(k):
-        ring_loss(k).wait_send()
-
-    for k in range(1, NV):
-        st(st_t, tt_s, tt_r, k).wait_send()
-        st(st_z, zz_s, zz_r, k).wait_send()
-        st(l_xy, lx_s, lx_r, k).wait_send()
-        gh_in(k).wait_send()
 
 
 def hand_over(loss, gh, gw, loss_out, gh_out, gw_out, sems):
@@ -531,7 +598,8 @@
     NB = 2 * NS
     W = V // NB
     RB = D // (2 * Z)
-    NE, NC, NG = (Z - 1) * NS, Z * NS, (Z - 2) * NS // 2
+    NA = NS // 2
+    NC, NG = Z * NA, (Z - 2) * NA
     vmem, dma = pltpu.VMEM, pltpu.SemaphoreType.DMA
     hbm = pl.BlockSpec(memory_space=pltpu.HBM)
     local = pl.BlockSpec(memory_space=pltpu.VMEM)
@@ -553,11 +621,11 @@
             vmem((NB, T, W), F32),
             vmem((NB, T, W), F32),
             vmem((NB, T, W), BF16),
-            vmem((2, 2, 2, RB, W), F32),
-            vmem((2, NC, RB, W), BF16),
-            vmem((2, NC, RB, W), BF16),
-            vmem((2, NE, RB, W), BF16),
-            vmem((2, NE, RB, W), BF16),
+            vmem((2, 2, 2, 2, RB, W), F32),
+            vmem((2, Z, NS, RB, W), BF16),
+            vmem((2, Z, NS, RB, W), BF16),
+            vmem((2, Z - 1, NS, RB, W), BF16),
+            vmem((2, Z - 1, NS, RB, W), BF16),
             vmem((NV, RB, T), BF16),
             vmem((NV, RB, T), BF16),
             vmem((4 * RB, T), F32),
@@ -581,7 +649,9 @@
             dma((2, NG)), dma((2, NG)),
             dma((2, NS)), dma((2, NS)),
             dma((2,)),
-            dma((2, NE)), dma((2, NE)),
+            dma((2, NS)), dma((2, NS)),
+            dma((2, NC)), dma((2, NC)),
+            dma((2, NS)), dma((2, NS)),
             dma((2, NC)), dma((2, NC)),
             dma((NV,)), dma((NV,)),
             dma((NV,)), dma((NV,)),
@@ -591,7 +661,7 @@
             dma((2,)),
         ],
         compiler_params=pltpu.CompilerParams(
-            collective_id=0, has_side_effects=True, vmem_limit_bytes=58 * 1024 * 1024
+            collective_id=0, has_side_effects=True, vmem_limit_bytes=60 * 1024 * 1024
         ),
         name="step",
     )(hidden, head, target, ids.reshape(1, T))

time: 115 us -> 110 us (0.957)
  Pallas kernels: 114 us -> 110 us
    pallas_call x1, Pallas kernels: 113 us -> 108 us  [body(): pl.pallas_call(functools.partial(kernel, dims), out_shape=(vmem((8, 128),...]
where the time goes in v3:
time: 110 us
  Pallas kernels  110 us (100%)
    pallas_call x1, Pallas kernels, body(): pl.pallas_call(functools.partial(kernel, dims), out_shape=(vmem((8, 128),...  108 us

profile of v3, /device:TPU:1, one launch (start us, length us, event | category | flops | bytes accessed | tf_op | source)
XLA Modules:
  0.0 110.3 jit_solution(10182649574045109410)
XLA Ops:
  0.6 108.1 %step.1 = (f32[8,128]{1,0:T(8,128)S(1)}, f32[64,512]{1,0:T(8,128)S(1)}, f32[64,4096]{1,0:T(8,128)S(1)}) custom-call(bf16[512,1024]{1,0:T(8,128)(2,1)} %refs_0_.1, bf16[64,4096]{1,0:T(8,128)(2,1)} %refs_1_.1, bf16[512,4096]{1,0:T(8,128)(2,1)} %refs_2_.1, s32[1,512]{1,0:T(1,128)} %bitcast.3), custom_call_target="tpu_custom_call" | custom-call | tf_op jit(solution)/shard_map/step/pallas_call | solution.py:606
  108.8 1.5 %hand_over.1 = (f32[1,1]{1,0:T(1,128)}, f32[64,512]{1,0:T(8,128)}, f32[64,4096]{1,0:T(8,128)}) custom-call(f32[8,128]{1,0:T(8,128)S(1)} %get-tuple-element.9.loss, f32[64,512]{1,0:T(8,128)S(1)} %get-tuple-element.10.gh, f32[64,4096]{1,0:T(8,128)S(1)} %get-tuple-element.11.gw), custom_call_target="tpu_custom_call" | custom-call | tf_op jit(solution)/shard_map/hand_over/pallas_call | solution.py:668

commit v4 on v3

--- a/solution.py
+++ b/solution.py
@@ -15,7 +15,7 @@
 BF16 = jnp.bfloat16
 MESH = pl.DeviceIdType.MESH
 ROWS = 32
-UNROLL = 4
+UNROLL = 8
 LOW = -1e30
 
 
@@ -51,9 +51,12 @@
     toward = ({"tok_0": right}, {"tok_0": left})
     other = {"tok_1": sib}
 
+    steps = [(dx, dy) for dx in range(X) for dy in range(Y) if dx or dy]
+    steps.sort(key=lambda d: -min(d[0], X - d[0]) - min(d[1], Y - d[1]))
+
     def plane(k):
-        j = lax.rem(me + k, NV)
-        return j, {"voc_0": j // Y, "voc_1": lax.rem(j, Y)}
+        px, py = lax.rem(x + steps[k - 1][0], X), lax.rem(y + steps[k - 1][1], Y)
+        return px * Y + py, {"voc_0": px, "voc_1": py}
 
     def remote(src, dst, s, r, device):
         return pltpu.make_async_remote_copy(
@@ -80,54 +83,88 @@
         for way in range(2):
             in_head(way * NS + i).start()
     in_ids.start()
+
+    barrier = pltpu.get_barrier_semaphore()
+    def tell(sem, device):
+        pl.semaphore_signal(sem, inc=1, device_id=device, device_id_type=MESH)
+
+    below_x, below_y = {"voc_0": x - 1}, {"voc_1": y - 1}
+    for device in (*toward, other):
+        tell(barrier, device)
+
+    @pl.when(x < X - 1)
+    def _():
+        tell(barrier, {"voc_0": x + 1})
+
+    @pl.when((x == 0) & (y < Y - 1))
+    def _():
+        tell(barrier, {"voc_1": y + 1})
+
+    pl.semaphore_wait(barrier, 3 + jnp.where((x > 0) | (y > 0), 1, 0))
+
+    def word(n):
+        @pl.when((x > 0) & (n == X - 1 - x))
+        def _():
+            @pl.when(x < X - 1)
+            def _():
+                pl.semaphore_wait(ready.at[0], 1)
+
+            tell(ready.at[0], below_x)
+
+        @pl.when((x == 0) & (n == X - 1))
+        def _():
+            pl.semaphore_wait(ready.at[0], 1)
+
+        @pl.when((x == 0) & (y > 0) & (n == X - 1 + Y - 1 - y))
+        def _():
+            @pl.when(y < Y - 1)
+            def _():
+                pl.semaphore_wait(ready.at[1], 1)
+
+            tell(ready.at[1], below_y)
+
+        @pl.when((me == 0) & (n == X - 1 + Y - 1))
+        def _():
+            pl.semaphore_wait(ready.at[1], 1)
+            for k in range(1, NV):
+                tell(ready.at[2], plane(k)[1])
+
+    def chip_at(way, s):
+        return lax.rem(z + Z - s, Z) if way == 0 else lax.rem(z + s, Z)
+
+    def pair(way, n, s, core):
+        return hg.at[2 * chip_at(way, s) + core, pl.ds(way * NS + 2 * lax.rem(n, NA), 2)]
+
+    def ag(way, n, s):
+        slot = pair(way, n, s, c)
+        return remote(slot, slot, ag_s.at[way, n], ag_r.at[way, n], toward[way])
+
+    def sb(way, n, core):
+        slot = pair(way, n, n // NA + 1, core)
+        return remote(slot, slot, sb_s.at[way, n], sb_r.at[way, n], other)
+
+    def al(way, i, s):
+        slot = hg.at[2 * chip_at(way, s) + c, way * NS + i]
+        return remote(slot, slot, al_s.at[way, i], al_r.at[way, i], toward[way])
+
+    def sl(way, i, core):
+        slot = hg.at[2 * chip_at(way, Z - 1) + core, way * NS + i]
+        return remote(slot, slot, sl_s.at[way, i], sl_r.at[way, i], other)
+
+    def shard(core):
+        slot = hg.at[2 * z + core]
+        return remote(slot, slot, so_sem.at[0], so_sem.at[1], other)
+
+    for i in range(NA):
+        for way in range(2):
+            for e in range(2):
+                in_head(way * NS + 2 * i + e).wait()
+            ag(way, i, 0).start()
+    shard(c).start()
     for k in range(Z):
         in_hid(k).start()
     for b in range(NB):
         in_tgt(b).start()
-
-    barrier = pltpu.get_barrier_semaphore()
-    row = [{"voc_0": lax.rem(x + k, X)} for k in range(1, X)]
-    line = [{"voc_1": lax.rem(y + k, Y)} for k in range(1, Y)]
-    near = (*toward, other, *row, *line)
-    for device in near:
-        pl.semaphore_signal(barrier, inc=1, device_id=device, device_id_type=MESH)
-    pl.semaphore_wait(barrier, len(near))
-
-    def chip_at(way, s):
-        return lax.rem(z + Z - s, Z) if way == 0 else lax.rem(z + s, Z)
-
-    def pair(way, n, s, core):
-        return hg.at[2 * chip_at(way, s) + core, pl.ds(way * NS + 2 * lax.rem(n, NA), 2)]
-
-    def ag(way, n, s):
-        slot = pair(way, n, s, c)
-        return remote(slot, slot, ag_s.at[way, n], ag_r.at[way, n], toward[way])
-
-    def sb(way, n, core):
-        slot = pair(way, n, n // NA + 1, core)
-        return remote(slot, slot, sb_s.at[way, n], sb_r.at[way, n], other)
-
-    def al(way, i, s):
-        slot = hg.at[2 * chip_at(way, s) + c, way * NS + i]
-        return remote(slot, slot, al_s.at[way, i], al_r.at[way, i], toward[way])
-
-    def sl(way, i, core):
-        slot = hg.at[2 * chip_at(way, Z - 1) + core, way * NS + i]
-        return remote(slot, slot, sl_s.at[way, i], sl_r.at[way, i], other)
-
-    def shard(core):
-        slot = hg.at[2 * z + core]
-        return remote(slot, slot, so_sem.at[0], so_sem.at[1], other)
-
-    for i in range(NA):
-        for way in range(2):
-            for e in range(2):
-                in_head(way * NS + 2 * i + e).wait()
-            ag(way, i, 0).start()
-    shard(c).start()
-    for device in row:
-        pl.semaphore_signal(ready, inc=1, device_id=device, device_id_type=MESH)
-
     @pl.loop(0, NB)
     def _(b):
         zed[b] = jnp.zeros((T, W), F32)
@@ -262,13 +299,18 @@
                 for way in range(2):
                     stats(lambda at: tgt[way * NS + 2 * i + e, at].astype(F32))
 
-        @pl.when((s == 3) & (i == 0))
-        def _():
-            pl.semaphore_wait(ready, X - 1)
+        word(n)
+
+        @pl.when(n == X + Y - 1)
+        def _():
+            @pl.when(me > 0)
+            def _():
+                pl.semaphore_wait(ready.at[2], 1)
+
             send_stats(st_t, tt_s, tt_r)
             reset()
 
-        @pl.when((s == 4) & (i == NA - 1))
+        @pl.when(n == X + Y + 1)
         def _():
             top, total = joined_stats(st_t, tt_s, tt_r)
             m_c[...] = column(top)
@@ -359,35 +401,38 @@
 
     def finish(n):
         s = n // NA
+        first = 2 * lax.rem(n, NA)
+        own = part.at[lax.rem(n, 2)]
         for way in range(2):
             rb(way, n).wait_recv()
+            for e in range(2):
+                own[way, e, c] += sib_in[way, s, first + e].astype(F32)
+
+        def joined(way, e):
+            return own[way, e, c] + ring_in[way, s - 1, first + e].astype(F32)
+
+        for way in range(2):
 
             @pl.when(s == 1)
             def _():
                 for e in range(2):
-                    rl(way, 2 * lax.rem(n, NA) + e).wait_recv()
+                    rl(way, first + e).wait_recv()
 
             @pl.when(s > 1)
             def _():
                 rs(way, n - NA).wait_recv()
 
-            for e in range(2):
-                i = 2 * lax.rem(n, NA) + e
-                own = part[lax.rem(n, 2), way, e, c] + sib_in[way, s, i].astype(F32)
-                val = own + ring_in[way, s - 1, i].astype(F32)
-
-                @pl.when(s < Z - 1)
-                def _():
-                    ring_out[way, s, i] = val.astype(BF16)
-
-                @pl.when(s == Z - 1)
-                def _():
-                    at = pl.ds(pl.multiple_of((way * NS + i) * W, W), W)
-                    gw_out[:, at] = val
-
             @pl.when(s < Z - 1)
             def _():
+                for e in range(2):
+                    ring_out[way, s, first + e] = joined(way, e).astype(BF16)
                 rs(way, n).start()
+
+            @pl.when(s == Z - 1)
+            def _():
+                for e in range(2):
+                    at = pl.ds(pl.multiple_of((way * NS + first + e) * W, W), W)
+                    gw_out[:, at] = joined(way, e)
 
     def gh(j):
         device = {"voc_0": j // Y, "voc_1": lax.rem(j, Y)}
@@ -643,7 +688,7 @@
             vmem((2, 8, 128), F32),
             vmem((Z, 8, 128), F32),
             dma((2 * NB + Z + 1,)),
-            pltpu.SemaphoreType.REGULAR,
+            pltpu.SemaphoreType.REGULAR((3,)),
             dma((2, NG)), dma((2, NG)),
             dma((2, NS)), dma((2, NS)),
             dma((2, NG)), dma((2, NG)),

time: 110 us -> 110 us (level)
  no operation moved by 1% of the time
where the time goes in v4:
time: 110 us
  Pallas kernels  109 us (99%)
    pallas_call x1, Pallas kernels, body(): pl.pallas_call(functools.partial(kernel, dims), out_shape=(vmem((8, 128),...  107 us

profile of v4, /device:TPU:1, one launch (start us, length us, event | category | flops | bytes accessed | tf_op | source)
XLA Modules:
  0.0 109.6 jit_solution(10847851982694125282)
XLA Ops:
  0.6 107.4 %step.1 = (f32[8,128]{1,0:T(8,128)S(1)}, f32[64,512]{1,0:T(8,128)S(1)}, f32[64,4096]{1,0:T(8,128)S(1)}) custom-call(bf16[512,1024]{1,0:T(8,128)(2,1)} %refs_0_.1, bf16[64,4096]{1,0:T(8,128)(2,1)} %refs_1_.1, bf16[512,4096]{1,0:T(8,128)(2,1)} %refs_2_.1, s32[1,512]{1,0:T(1,128)} %bitcast.3), custom_call_target="tpu_custom_call" | custom-call | tf_op jit(solution)/shard_map/step/pallas_call | solution.py:651
  108.1 1.5 %hand_over.1 = (f32[1,1]{1,0:T(1,128)}, f32[64,512]{1,0:T(8,128)}, f32[64,4096]{1,0:T(8,128)}) custom-call(f32[8,128]{1,0:T(8,128)S(1)} %get-tuple-element.9.loss, f32[64,512]{1,0:T(8,128)S(1)} %get-tuple-element.10.gh, f32[64,4096]{1,0:T(8,128)S(1)} %get-tuple-element.11.gw), custom_call_target="tpu_custom_call" | custom-call | tf_op jit(solution)/shard_map/hand_over/pallas_call | solution.py:713
